TPU v7x, 32 devices: a whole 2x2x4 slice. The times are simulated.
32 devices in a mesh: rep: 2 (over x), dp: 16 (over y, z, core).
Axes of the slice: x: 2, y: 2, z: 4, core: 2. Of those that a mesh axis runs over, the one named last changes fastest.
Arguments:
- x: bfloat16 [32, 2048, 1024], P(('rep', 'dp')), parts along dimension 0
- dy: bfloat16 [32, 2048, 1024], P(('rep', 'dp')), parts along dimension 0
- w_gate: bfloat16 [2, 1024, 3200], P(None, 'dp')
- w_up: bfloat16 [2, 1024, 3200], P(None, 'dp')
- w_down: bfloat16 [2, 3200, 1024], P(None, 'dp')
- m_w_gate: float32 [2, 1024, 3200], P(None, 'dp')
- m_w_up: float32 [2, 1024, 3200], P(None, 'dp')
- m_w_down: float32 [2, 3200, 1024], P(None, 'dp')
- v_w_gate: float32 [2, 1024, 3200], P(None, 'dp')
- v_w_up: float32 [2, 1024, 3200], P(None, 'dp')
- v_w_down: float32 [2, 3200, 1024], P(None, 'dp')
Outputs:
- output 1: bfloat16 [4, 1024, 3200], P('rep', 'dp'), parts along dimension 0
- output 2: bfloat16 [4, 1024, 3200], P('rep', 'dp'), parts along dimension 0
- output 3: bfloat16 [4, 3200, 1024], P('rep', 'dp'), parts along dimension 0
- output 4: float32 [4, 1024, 3200], P('rep', 'dp'), parts along dimension 0
- output 5: float32 [4, 1024, 3200], P('rep', 'dp'), parts along dimension 0
- output 6: float32 [4, 3200, 1024], P('rep', 'dp'), parts along dimension 0
- output 7: float32 [4, 1024, 3200], P('rep', 'dp'), parts along dimension 0
- output 8: float32 [4, 1024, 3200], P('rep', 'dp'), parts along dimension 0
- output 9: float32 [4, 3200, 1024], P('rep', 'dp'), parts along dimension 0
There are 2 independent parts. A program takes and returns all parts, laid end to end along the dimension named above; an argument that names none is the same for every part.
All inputs are finite; a program needn't handle non-finite values.
Results may differ from a plain program's by a relative error of at most 0.022.
Values are sent between devices in bfloat16 or wider.
A program may use at most 2 GiB of HBM per device.

v0:
```python
import jax
import jax.numpy as jnp
from jax import lax
from jax.sharding import PartitionSpec as P

NAMES = ("w_gate", "w_up", "w_down")


def matmul(a, w):
    return jnp.dot(a, w, preferred_element_type=jnp.float32).astype(jnp.bfloat16)


def normed(h):
    wide = h.astype(jnp.float32)
    scale = lax.rsqrt(jnp.mean(wide**2, -1, keepdims=True) + 1e-6)
    return (wide * scale).astype(jnp.bfloat16)


def layer(h, w):
    a = normed(h)
    gate = jnp.dot(a, w["w_gate"], preferred_element_type=jnp.float32)
    up = jnp.dot(a, w["w_up"], preferred_element_type=jnp.float32)
    return h + matmul((jax.nn.silu(gate) * up).astype(jnp.bfloat16), w["w_down"])


def adamw(w, m, v, g):
    m = 0.9 * m + 0.1 * g
    v = 0.95 * v + 0.05 * g * g
    step = m * lax.rsqrt(v + 1e-8) + 0.1 * w
    return (w - 0.02 * step).astype(jnp.bfloat16), m, v


def solution(mesh):
    def fetched(weights, number):
        return {name: lax.all_gather(w[number], "dp", axis=0, tiled=True) for name, w in zip(NAMES, weights, strict=True)}

    def step(x, dy, *arrays):
        weights, m, v = (arrays[i : i + 3] for i in (0, 3, 6))
        layers = weights[0].shape[0]
        h, kept = x[0], []
        for number in range(layers):
            kept.append(h)
            h = layer(h, fetched(weights, number))
        by_h, mine = dy[0], [None] * layers
        for number in reversed(range(layers)):
            _, back = jax.vjp(lambda w, h: layer(h, w), fetched(weights, number), kept[number])
            by_w, by_h = back(by_h)
            mine[number] = [lax.psum_scatter(by_w[name], "dp", scatter_dimension=0, tiled=True) for name in NAMES]
        gradients = [jnp.stack([mine[number][i] for number in range(layers)]).astype(jnp.float32) for i in range(3)]
        new = [adamw(w.astype(jnp.float32), m, v, g) for w, m, v, g in zip(weights, m, v, gradients, strict=True)]
        return tuple(one[which] for which in range(3) for one in new)

    states, cut = P(("rep", "dp"), None, None), P(None, "dp", None)
    return jax.shard_map(
        step,
        mesh=mesh,
        in_specs=(states, states) + (cut,) * 9,
        out_specs=(P("rep", "dp", None),) * 9,
        check_vma=False,
    )
```

profile of v0, /device:TPU:0, one launch (start us, length us, event | category | flops | bytes accessed | tf_op | source)
XLA Modules:
  0.0 1059.3 jit_solution(8459869252881653384)
XLA Ops:
  7.2 0.0 all-gather.13.cloned.1.call-start
  7.2 2.1 fusion.88
  9.3 0.0 all-gather.13.cloned.1.call-update
  9.3 0.0 all-gather.15.cloned.1.call-start
  9.4 2.1 fusion.87
  11.4 0.0 all-gather.15.cloned.1.call-update
  11.5 0.0 all-gather.17.cloned.1.call-start
  11.5 2.1 fusion.86
  13.6 0.0 all-gather.17.cloned.1.call-update
  13.6 0.0 all-gather.21.cloned.1.call-start
  13.7 0.5 all-gather.21.cloned.1.call-update
  14.2 0.0 all-gather.23.cloned.1.call-start
  14.2 0.5 all-gather.23.cloned.1.call-update
  14.8 0.0 all-gather.19.cloned.1.call-start
  14.8 0.5 all-gather.19.cloned.1.call-update
  15.3 0.0 reduce-scatter.15.cloned.1.call-start
  15.4 6.6 copy.20
  22.0 3.1 fusion.15
  25.0 6.5 copy.21
  31.6 44.9 %all-gather.13.cloned.1.call-done = bf16[1,1024,3200]{2,1,0:T(8,128)(2,1)} async-done(((bf16[1,64,3200]{2,1,0:T(8,128)(2,1)}), bf16[1,1024,3200]{2,1,0:T(8,128)(2,1)}) %all-gather.13.cloned.1.call-update) | async-done | bytes 6553616 | tf_op jit(solution)/shard_map/all_gather | solution.py:35
  76.5 22.9 %fusion.41 = f32[2048,3200]{1,0:T(8,128)} fusion(bf16[1,1024,3200]{2,1,0:T(8,128)(2,1)} %all-gather.13.cloned.1.call-done, bf16[1,2048,1024]{1,2,0:T(8,128)(2,1)} %copy.20, f32[2048]{0:T(1024)S(1)} %add_rsqrt_fusion), kind=kOutput, calls=%fused_computation.59 | convolution fusion | flops 13428064256 | bytes 36970496 | tf_op jit(solution)/shard_map/dot_general | solution.py:21
  99.4 42.1 %all-gather.15.cloned.1.call-done = bf16[1,1024,3200]{2,1,0:T(8,128)(2,1)} async-done(((bf16[1,64,3200]{2,1,0:T(8,128)(2,1)}), bf16[1,1024,3200]{2,1,0:T(8,128)(2,1)}) %all-gather.15.cloned.1.call-update) | async-done | bytes 6553616 | tf_op jit(solution)/shard_map/all_gather | solution.py:35
  141.4 31.4 %multiply_convert_fusion.1 = (bf16[2048,3200]{1,0:T(8,128)(2,1)}, f32[2048,3200]{1,0:T(8,128)}) fusion(f32[2048,3200]{1,0:T(8,128)} %fusion.41, bf16[1,1024,3200]{2,1,0:T(8,128)(2,1)} %all-gather.15.cloned.1.call-done, bf16[1,2048,1024]{1,2,0:T(8,128)(2,1)} %copy.20, f32[2048]{0:T(1024)S(1)} %add_rsqrt_fusion), kind=kOutput, calls=%fused_computation.17 | convolution fusion | flops 13467385856 | bytes 76292096 | tf_op jit(solution)/shard_map/dot_general | solution.py:22
  172.8 33.6 %all-gather.17.cloned.1.call-done = bf16[1,3200,1024]{2,1,0:T(8,128)(2,1)} async-done(((bf16[1,200,1024]{2,1,0:T(8,128)(2,1)}), bf16[1,3200,1024]{2,1,0:T(8,128)(2,1)}) %all-gather.17.cloned.1.call-update) | async-done | bytes 6553616 | tf_op jit(solution)/shard_map/all_gather | solution.py:35
  206.4 21.9 %fusion.19 = (f32[2048]{0:T(1024)S(1)}, bf16[2048,1024]{0,1:T(8,128)(2,1)}) fusion(bf16[2048,3200]{1,0:T(8,128)(2,1)} %get-tuple-element.24, bf16[1,3200,1024]{2,1,0:T(8,128)(2,1)} %all-gather.17.cloned.1.call-done, bf16[1,2048,1024]{1,2,0:T(8,128)(2,1)} %copy.20), kind=kOutput, calls=%fused_computation.37 | convolution fusion | flops 13432256512 | bytes 28057600 | tf_op jit(solution)/shard_map/dot_general | solution.py:10
  228.3 0.0 copy-start.9
  228.3 42.9 %all-gather.21.cloned.1.call-done = bf16[1,3200,1024]{2,1,0:T(8,128)(2,1)} async-done(((bf16[1,200,1024]{2,1,0:T(8,128)(2,1)}), bf16[1,3200,1024]{2,1,0:T(8,128)(2,1)}) %all-gather.21.cloned.1.call-update) | async-done | bytes 6553616 | tf_op jit(solution)/shard_map/all_gather | solution.py:35
  271.2 20.9 %convolution_convert_fusion.1 = bf16[2048,3200]{1,0:T(8,128)(2,1)} fusion(bf16[1,3200,1024]{2,1,0:T(8,128)(2,1)} %all-gather.21.cloned.1.call-done, bf16[1,2048,1024]{2,1,0:T(8,128)(2,1)} %param.12), kind=kOutput, calls=%fused_computation.23 | convolution fusion | flops 13428326400 | bytes 23855104 | tf_op jit(solution)/shard_map/transpose(jvp())/dot_general | solution.py:10
  292.1 43.9 %all-gather.23.cloned.1.call-done = bf16[1,1024,3200]{2,1,0:T(8,128)(2,1)} async-done(((bf16[1,64,3200]{2,1,0:T(8,128)(2,1)}), bf16[1,1024,3200]{2,1,0:T(8,128)(2,1)}) %all-gather.23.cloned.1.call-update) | async-done | bytes 6553616 | tf_op jit(solution)/shard_map/all_gather | solution.py:35
  336.0 22.8 %fusion.28 = f32[2048,3200]{1,0:T(8,128)} fusion(bf16[1,1024,3200]{2,1,0:T(8,128)(2,1)} %all-gather.23.cloned.1.call-done, bf16[2048,1024]{0,1:T(8,128)(2,1)} %get-tuple-element.27, f32[2048]{0:T(1024)S(1)} %fusion.74), kind=kOutput, calls=%fused_computation.46 | convolution fusion | flops 13428064256 | bytes 36970496 | tf_op jit(solution)/shard_map/jvp()/dot_general | solution.py:22
  358.8 42.0 %all-gather.19.cloned.1.call-done = bf16[1,1024,3200]{2,1,0:T(8,128)(2,1)} async-done(((bf16[1,64,3200]{2,1,0:T(8,128)(2,1)}), bf16[1,1024,3200]{2,1,0:T(8,128)(2,1)}) %all-gather.19.cloned.1.call-update) | async-done | bytes 6553616 | tf_op jit(solution)/shard_map/all_gather | solution.py:35
  400.9 38.7 %fusion.2 = (bf16[2048,3200]{1,0:T(8,128)(2,1)}, f32[2048,3200]{1,0:T(8,128)}) fusion(f32[2048,3200]{1,0:T(8,128)} %fusion.28, bf16[2048,3200]{1,0:T(8,128)(2,1)} %convolution_convert_fusion.1, bf16[1,1024,3200]{2,1,0:T(8,128)(2,1)} %all-gather.19.cloned.1.call-done, bf16[2048,1024]{0,1:T(8,128)(2,1)} %get-tuple-element.27, f32[2048]{0:T(1024)S(1)} %fusion.74), kind=kOutput, calls=%fused_computation.8 | convolution fusion | flops 13506707456 | bytes 89399296 | tf_op jit(solution)/shard_map/jvp()/dot_general | solution.py:21
  439.6 22.6 %fusion.12 = bf16[2048,1024]{0,1:T(8,128)(2,1)} fusion(bf16[2048,3200]{1,0:T(8,128)(2,1)} %convolution_convert_fusion.1, bf16[1,1024,3200]{2,1,0:T(8,128)(2,1)} %all-gather.23.cloned.1.call-done, f32[2048,3200]{1,0:T(8,128)} %get-tuple-element.29), kind=kOutput, calls=%fused_computation.21 | convolution fusion | flops 13461094400 | bytes 50069504 | tf_op jit(solution)/shard_map/transpose(jvp())/dot_general | solution.py:22
  462.2 21.8 %fusion.21 = (f32[2048]{0:T(1024)S(1)}, bf16[2048,1024]{0,1:T(8,128)(2,1)}) fusion(bf16[2048,1024]{0,1:T(8,128)(2,1)S(1)} %copy-done.2, bf16[2048,1024]{0,1:T(8,128)(2,1)} %fusion.12, bf16[2048,3200]{1,0:T(8,128)(2,1)} %get-tuple-element.28, bf16[1,1024,3200]{2,1,0:T(8,128)(2,1)} %all-gather.19.cloned.1.call-done), kind=kOutput, calls=%fused_computation.39 | convolution fusion | flops 13432256512 | bytes 32251904 | tf_op jit(solution)/shard_map/transpose(jvp())/dot_general | solution.py:21
  484.0 4.9 fusion.44
  488.9 2.0 copy-done.3
  491.0 19.5 %convolution_convert_fusion.2 = bf16[3200,1024]{1,0:T(8,128)(2,1)} fusion(bf16[2048,3200]{1,0:T(8,128)(2,1)} %get-tuple-element.24, bf16[2048,1024]{0,1:T(8,128)(2,1)S(1)} %fusion.44), kind=kOutput, calls=%fused_computation.44 | convolution fusion | flops 13425049600 | bytes 23855104 | tf_op jit(solution)/shard_map/transpose(jvp())/dot_general | solution.py:10
  510.4 0.0 reduce-scatter.15.cloned.1.call-update
  510.5 0.0 reduce-scatter.17.cloned.1.call-start
  510.5 26.0 %fusion.25 = bf16[3200,1024]{1,0:T(8,128)(2,1)} fusion(f32[2048,3200]{1,0:T(8,128)} %fusion.28, bf16[1,2048,1024]{2,1,0:T(8,128)(2,1)} %param.12, f32[2048,3200]{1,0:T(8,128)} %get-tuple-element.29), kind=kOutput, calls=%fused_computation.41 | convolution fusion | flops 13464371200 | bytes 63176704 | tf_op jit(solution)/shard_map/transpose(jvp())/dot_general | solution.py:10
  536.5 0.0 reduce-scatter.17.cloned.1.call-update
  536.6 0.0 reduce-scatter.11.cloned.1.call-start
  536.6 21.4 %convolution_convert_fusion = bf16[2048,3200]{1,0:T(8,128)(2,1)} fusion(bf16[2048,1024]{0,1:T(8,128)(2,1)} %copy-done.3, bf16[1,3200,1024]{2,1,0:T(8,128)(2,1)} %all-gather.17.cloned.1.call-done), kind=kOutput, calls=%fused_computation.22 | convolution fusion | flops 13428326400 | bytes 23855104 | tf_op jit(solution)/shard_map/transpose(jvp())/dot_general | solution.py:10
  558.1 24.3 %fusion.27 = bf16[1024,3200]{1,0:T(8,128)(2,1)} fusion(bf16[2048,3200]{1,0:T(8,128)(2,1)} %convolution_convert_fusion, f32[2048,3200]{1,0:T(8,128)} %fusion.41, bf16[1,2048,1024]{1,2,0:T(8,128)(2,1)S(1)} %copy-done.1, f32[2048]{0:T(1024)S(1)} %copy-done.14), kind=kOutput, calls=%fused_computation.43 | convolution fusion | flops 13470662656 | bytes 50077696 | tf_op jit(solution)/shard_map/transpose(jvp())/dot_general | solution.py:22
  582.4 0.0 reduce-scatter.11.cloned.1.call-update
  582.4 0.0 reduce-scatter.13.cloned.1.call-start
  582.5 0.6 copy-done.10
  583.1 25.3 %fusion.26 = bf16[1024,3200]{1,0:T(8,128)(2,1)} fusion(bf16[2048,3200]{1,0:T(8,128)(2,1)} %convolution_convert_fusion.1, bf16[2048,1024]{0,1:T(8,128)(2,1)} %get-tuple-element.27, f32[2048]{0:T(1024)S(1)} %copy-done.10, f32[2048,3200]{1,0:T(8,128)} %get-tuple-element.29), kind=kOutput, calls=%fused_computation.42 | convolution fusion | flops 13470662656 | bytes 50077696 | tf_op jit(solution)/shard_map/transpose(jvp())/dot_general | solution.py:22
  608.4 0.0 reduce-scatter.13.cloned.1.call-update
  608.4 0.0 reduce-scatter.7.cloned.1.call-start
  608.5 32.5 %fusion.22 = bf16[1024,3200]{1,0:T(8,128)(2,1)} fusion(f32[2048,3200]{1,0:T(8,128)} %fusion.41, f32[2048,3200]{1,0:T(8,128)} %get-tuple-element.25, bf16[2048,3200]{1,0:T(8,128)(2,1)} %convolution_convert_fusion, bf16[1,2048,1024]{1,2,0:T(8,128)(2,1)} %copy.20, f32[2048]{0:T(1024)S(1)} %copy-done.14), kind=kOutput, calls=%fused_computation.40 | convolution fusion | flops 13503430656 | bytes 76292096 | tf_op jit(solution)/shard_map/transpose(jvp())/dot_general | solution.py:21
  641.0 0.0 reduce-scatter.7.cloned.1.call-update
  641.0 0.0 reduce-scatter.9.cloned.1.call-start
  641.1 21.0 %convolution_convert_fusion.3 = bf16[1024,3200]{1,0:T(8,128)(2,1)} fusion(bf16[2048,3200]{1,0:T(8,128)(2,1)} %get-tuple-element.28, bf16[2048,1024]{0,1:T(8,128)(2,1)} %get-tuple-element.27, f32[2048]{0:T(1024)S(1)} %copy-done.10), kind=kOutput, calls=%fused_computation.45 | convolution fusion | flops 13428064256 | bytes 23863296 | tf_op jit(solution)/shard_map/transpose(jvp())/dot_general | solution.py:21
  662.1 0.0 reduce-scatter.9.cloned.1.call-update
  662.2 0.0 reduce-scatter.15.cloned.1.call-done
  662.2 25.0 %reduce-scatter.17.cloned.1.call-done = bf16[200,1024]{1,0:T(8,128)(2,1)} async-done(((bf16[3200,1024]{1,0:T(8,128)(2,1)}), bf16[200,1024]{1,0:T(8,128)(2,1)}) %reduce-scatter.17.cloned.1.call-update) | async-done | bytes 409616 | tf_op jit(solution)/shard_map/reduce_scatter | solution.py:48
  687.2 4.2 fusion.69
  691.4 86.3 %reduce-scatter.11.cloned.1.call-done = bf16[64,3200]{1,0:T(8,128)(2,1)} async-done(((bf16[1024,3200]{1,0:T(8,128)(2,1)}), bf16[64,3200]{1,0:T(8,128)(2,1)}) %reduce-scatter.11.cloned.1.call-update) | async-done | bytes 409616 | tf_op jit(solution)/shard_map/reduce_scatter | solution.py:48
  777.7 90.2 %reduce-scatter.13.cloned.1.call-done = bf16[64,3200]{1,0:T(8,128)(2,1)} async-done(((bf16[1024,3200]{1,0:T(8,128)(2,1)}), bf16[64,3200]{1,0:T(8,128)(2,1)}) %reduce-scatter.13.cloned.1.call-update) | async-done | bytes 409616 | tf_op jit(solution)/shard_map/reduce_scatter | solution.py:48
  867.9 4.6 fusion.65
  872.4 85.6 %reduce-scatter.7.cloned.1.call-done = bf16[64,3200]{1,0:T(8,128)(2,1)} async-done(((bf16[1024,3200]{1,0:T(8,128)(2,1)}), bf16[64,3200]{1,0:T(8,128)(2,1)}) %reduce-scatter.7.cloned.1.call-update) | async-done | bytes 409616 | tf_op jit(solution)/shard_map/reduce_scatter | solution.py:48
  958.1 90.1 %reduce-scatter.9.cloned.1.call-done = bf16[64,3200]{1,0:T(8,128)(2,1)} async-done(((bf16[1024,3200]{1,0:T(8,128)(2,1)}), bf16[64,3200]{1,0:T(8,128)(2,1)}) %reduce-scatter.9.cloned.1.call-update) | async-done | bytes 409616 | tf_op jit(solution)/shard_map/reduce_scatter | solution.py:48
  1048.1 4.1 fusion.61
  (30 shorter events, 0.1 us)
Async XLA Ops:
  7.2 69.3 %all-gather.13.cloned.1.call-start = ((), (), s32[]{:S(2)}) async-start(), calls=%async_computation.12 | async-start | bytes 6963200 | tf_op jit(solution)/shard_map/all_gather | solution.py:35
  9.3 132.1 %all-gather.15.cloned.1.call-start = ((), (), s32[]{:S(2)}) async-start(), calls=%async_computation.13 | async-start | bytes 6963200 | tf_op jit(solution)/shard_map/all_gather | solution.py:35
  11.5 194.9 %all-gather.17.cloned.1.call-start = ((), (), s32[]{:S(2)}) async-start(), calls=%async_computation.14 | async-start | bytes 6963200 | tf_op jit(solution)/shard_map/all_gather | solution.py:35
  13.6 257.6 %all-gather.21.cloned.1.call-start = ((), (), s32[]{:S(2)}) async-start(), calls=%async_computation.16 | async-start | bytes 6963200 | tf_op jit(solution)/shard_map/all_gather | solution.py:35
  14.2 321.8 %all-gather.23.cloned.1.call-start = ((), (), s32[]{:S(2)}) async-start(), calls=%async_computation.17 | async-start | bytes 6963200 | tf_op jit(solution)/shard_map/all_gather | solution.py:35
  14.8 386.1 %all-gather.19.cloned.1.call-start = ((), (), s32[]{:S(2)}) async-start(), calls=%async_computation.15 | async-start | bytes 6963200 | tf_op jit(solution)/shard_map/all_gather | solution.py:35
  15.3 646.8 %reduce-scatter.15.cloned.1.call-start = ((), (), s32[]{:S(2)}) async-start(), calls=%async_computation.10 | async-start | bytes 6963200 | tf_op jit(solution)/shard_map/reduce_scatter | solution.py:48
  25.0 116.4 %copy-start.13 = (f32[2048]{0:T(1024)}, f32[2048]{0:T(1024)S(1)}, u32[]{:S(2)}) copy-start(f32[2048]{0:T(1024)S(1)} %add_rsqrt_fusion) | copy-start | bytes 24580
  228.3 63.8 %copy-start.11 = (f32[2048]{0:T(1024)}, f32[2048]{0:T(1024)S(1)}, u32[]{:S(2)}) copy-start(f32[2048]{0:T(1024)S(1)} %get-tuple-element.26) | copy-start | bytes 24580
  228.3 255.7 %copy-start.9 = (f32[2048]{0:T(1024)}, f32[2048]{0:T(1024)S(1)}, u32[]{:S(2)}) copy-start(f32[2048]{0:T(1024)S(1)} %fusion.74) | copy-start | bytes 24580
  439.6 22.6 %copy-start.2 = (bf16[2048,1024]{0,1:T(8,128)(2,1)S(1)}, bf16[2048,1024]{0,1:T(8,128)(2,1)}, u32[]{:S(2)}) copy-start(bf16[2048,1024]{0,1:T(8,128)(2,1)} %get-tuple-element.27) | copy-start | bytes 12582916
  462.2 21.8 %copy-start.12 = (f32[2048]{0:T(1024)S(1)}, f32[2048]{0:T(1024)}, u32[]{:S(2)}) copy-start(f32[2048]{0:T(1024)} %copy-done.11) | copy-start | bytes 24580
  462.2 21.8 %copy-start = (bf16[1,2048,1024]{1,2,0:T(8,128)(2,1)S(1)}, bf16[1,2048,1024]{1,2,0:T(8,128)(2,1)}, u32[]{:S(2)}) copy-start(bf16[1,2048,1024]{1,2,0:T(8,128)(2,1)} %copy.21) | copy-start | bytes 12582916
  488.9 2.0 copy-start.3
  510.5 176.7 %reduce-scatter.17.cloned.1.call-start = ((), (), s32[]{:S(2)}) async-start(), calls=%async_computation.11 | async-start | bytes 6963200 | tf_op jit(solution)/shard_map/reduce_scatter | solution.py:48
  536.6 21.5 %copy-start.14 = (f32[2048]{0:T(1024)S(1)}, f32[2048]{0:T(1024)}, u32[]{:S(2)}) copy-start(f32[2048]{0:T(1024)} %copy-done.13) | copy-start | bytes 24580
  536.6 241.1 %reduce-scatter.11.cloned.1.call-start = ((), (), s32[]{:S(2)}) async-start(), calls=%async_computation.8 | async-start | bytes 6963200 | tf_op jit(solution)/shard_map/reduce_scatter | solution.py:48
  536.6 21.5 %copy-start.1 = (bf16[1,2048,1024]{1,2,0:T(8,128)(2,1)S(1)}, bf16[1,2048,1024]{1,2,0:T(8,128)(2,1)}, u32[]{:S(2)}) copy-start(bf16[1,2048,1024]{1,2,0:T(8,128)(2,1)} %copy.20) | copy-start | bytes 12582916
  582.4 0.7 copy-start.10
  582.4 285.4 %reduce-scatter.13.cloned.1.call-start = ((), (), s32[]{:S(2)}) async-start(), calls=%async_computation.9 | async-start | bytes 6963200 | tf_op jit(solution)/shard_map/reduce_scatter | solution.py:48
  608.4 349.6 %reduce-scatter.7.cloned.1.call-start = ((), (), s32[]{:S(2)}) async-start(), calls=%async_computation.6 | async-start | bytes 6963200 | tf_op jit(solution)/shard_map/reduce_scatter | solution.py:48
  641.0 407.1 %reduce-scatter.9.cloned.1.call-start = ((), (), s32[]{:S(2)}) async-start(), calls=%async_computation.7 | async-start | bytes 6963200 | tf_op jit(solution)/shard_map/reduce_scatter | solution.py:48
  662.1 25.1 %copy-start.4 = (bf16[2,200,1024]{2,1,0:T(8,128)(2,1)S(1)}, bf16[2,200,1024]{2,1,0:T(8,128)(2,1)}, u32[]{:S(2)}) copy-start(bf16[2,200,1024]{2,1,0:T(8,128)(2,1)} %param.15) | copy-start | bytes 2457604
  662.1 25.1 %copy-start.7 = (f32[2,200,1024]{2,1,0:T(8,128)S(1)}, f32[2,200,1024]{2,1,0:T(8,128)}, u32[]{:S(2)}) copy-start(f32[2,200,1024]{2,1,0:T(8,128)} %param.21) | copy-start | bytes 4915204
  662.1 205.7 %copy-start.5 = (bf16[2,64,3200]{2,1,0:T(8,128)(2,1)S(1)}, bf16[2,64,3200]{2,1,0:T(8,128)(2,1)}, u32[]{:S(2)}) copy-start(bf16[2,64,3200]{2,1,0:T(8,128)(2,1)} %param.14) | copy-start | bytes 2457604
  691.4 356.8 %copy-start.6 = (bf16[2,64,3200]{2,1,0:T(8,128)(2,1)S(1)}, bf16[2,64,3200]{2,1,0:T(8,128)(2,1)}, u32[]{:S(2)}) copy-start(bf16[2,64,3200]{2,1,0:T(8,128)(2,1)} %param.13) | copy-start | bytes 2457604
  691.4 356.8 %copy-start.8 = (f32[2,64,3200]{2,1,0:T(8,128)S(1)}, f32[2,64,3200]{2,1,0:T(8,128)}, u32[]{:S(2)}) copy-start(f32[2,64,3200]{2,1,0:T(8,128)} %param.19) | copy-start | bytes 4915204
Sparse Core Ops, SparseCore 0:
  10.9 65.5 all-gather.12
  79.3 62.0 all-gather.14
  144.3 62.0 all-gather.16
  209.1 62.0 all-gather.20
  274.0 62.0 all-gather.22
  338.8 62.0 all-gather.18
  510.6 86.2 reduce-scatter.14
  600.8 86.2 reduce-scatter.16
  691.2 86.4 reduce-scatter.10
  781.5 86.3 reduce-scatter.12
  871.8 86.1 reduce-scatter.6
  961.9 86.2 reduce-scatter.8
where the time goes:
time: 1070 us; the launch traced here: 1060 us
  waiting for transfers between devices  628 us (59%)
  matrix products  373 us (35%)
  local copies, waits for them, and re-layouts  22 us (2%)
  other arithmetic  20.8 us (2%)
  between operations  14.5 us (1%)
    reduce_scatter x6, waiting for transfers between devices, step(): lax.psum_scatter(by_w[name], 'dp', scatter_dimension=0, tiled=True)  377 us
    all_gather x6, waiting for transfers between devices, fetched(): lax.all_gather(w[number], 'dp', axis=0, tiled=True)  249 us
    dot_general x5, matrix products, layer(): gate = jnp.dot(a, w['w_gate'], preferred_element_type=jnp.float32)  137 us
    dot_general x5, matrix products, layer(): up = jnp.dot(a, w['w_up'], preferred_element_type=jnp.float32)  126 us
    dot_general x5, matrix products, matmul(): jnp.dot(a, w, preferred_element_type=jnp.float32).astype(jnp.bfloat16)  110 us
  transfers between devices with their start and end apart: 12, of which 11 were waited for; matrix products, arithmetic and copies ran while one was open for 28% of the time, Pallas kernels for 0%

commit v1 on v0

v1 whole, which is shorter than its diff:
```python
import functools

import jax
import jax.numpy as jnp
from jax import lax
from jax.experimental import pallas as pl
from jax.experimental.pallas import tpu as pltpu
from jax.sharding import PartitionSpec as P

NAMES = ("w_gate", "w_up", "w_down")
BF, WIDE = jnp.bfloat16, jnp.float32
MESH = pl.DeviceIdType.MESH
ANY = pl.BlockSpec(memory_space=pl.ANY)
VMEM = pltpu.VMEM
ROOM = 66_000_000
T, D, FF = 2048, 1024, 3200
RG, RD, PAD = D // 16, FF // 16, 208
TILE = 256
CHUNKS = ((0, 1024), (1024, 1024), (2048, 1152))


def adamw(w, m, v, g):
    m = 0.9 * m + 0.1 * g
    v = 0.95 * v + 0.05 * g * g
    step = m * lax.rsqrt(v + 1e-8) + 0.1 * w
    return (w - 0.02 * step).astype(BF), m, v


def dot(a, b, dims=((1,), (0,))):
    return lax.dot_general(a, b, (dims, ((), ())), preferred_element_type=WIDE)


def place():
    me = lax.axis_index("dp")
    return me // 8, me // 2 % 4, me % 2, lax.axis_index("rep")


def number(y, z, c):
    return (y * 4 + z) * 2 + c


def flip(bit):
    return 1 - bit


def xor4(z, k):
    low, high = z % 2, z // 2
    low = 1 - low if k % 2 else low
    high = 1 - high if k // 2 else high
    return high * 2 + low


def meet(barrier):
    y, z, c, x = place()
    peers = [{"dp": number(y, xor4(z, k), c)} for k in (1, 2, 3)]
    peers += [{"dp": number(1 - y, z, c)}, {"dp": number(y, z, 1 - c)}]
    return peers


def norm_scale(wide):
    return lax.rsqrt(jnp.mean(wide * wide, -1, keepdims=True) + 1e-6)


def put_hidden(hid_t, out):
    for i in range(16):
        out[i, 0:RD, :] = hid_t[i * RD : (i + 1) * RD, :].astype(BF)
        out[i, RD:PAD, :] = jnp.zeros((PAD - RD, TILE), BF)


class Gather:
    def __init__(self, base, layer, gu, wd, full, down, send, recv):
        self.y, self.z, self.c, self.x = place()
        self.layer, self.gu, self.wd, self.full, self.down, self.send, self.recv = layer, gu, wd, full, down, send, recv
        self.base = base

    def at(self, dy, k):
        return number(flip(self.y) if dy else self.y, xor4(self.z, k), self.c)

    def copy(self, which, stage, dy, k):
        kinds = ("Az", "Dz", "Ay", "Dy", "Ox", "Ac", "Oc", "Dc")
        sem = self.base + kinds.index(which + stage) * 8 + dy * 4 + k
        peer = {
            "z": lambda: {"dp": number(self.y, xor4(self.z, k), self.c)},
            "y": lambda: {"dp": number(1 - self.y, self.z, self.c)},
            "c": lambda: {"dp": number(self.y, self.z, 1 - self.c)},
            "x": lambda: {"rep": 1 - self.x},
        }[stage]()
        own = stage == "z" or (dy == 0 and k == 0)
        b = self.at(0, 0) if own else self.at(dy, k)
        if which == "D":
            dst = self.down.at[pl.ds(b * RD, RD), :]
            src = self.wd.at[self.layer] if own else dst
        else:
            m = 1 - self.x if which == "O" and stage == "c" else self.x
            dst = self.full.at[m, b]
            src = self.gu.at[m, self.layer] if own else dst
        return pltpu.make_async_remote_copy(
            src_ref=src, dst_ref=dst, send_sem=self.send.at[sem], recv_sem=self.recv.at[sem], device_id=peer, device_id_type=MESH
        )

    def begin(self):
        for k in (1, 2, 3):
            self.copy("A", "z", 0, k).start()
        self.copy("A", "y", 0, 0).start()
        for k in (1, 2, 3):
            self.copy("D", "z", 0, k).start()
        self.copy("D", "y", 0, 0).start()
        for which in "AOD":
            self.copy(which, "c", 0, 0).start()

    def passed_on(self, event):
        which, stage, dy, k = event
        self.copy(which, stage, dy, k).wait_recv()
        if stage == "z":
            self.copy(which, "y", 0, k).start()
            self.copy(which, "c", 0, k).start()
            if which == "A":
                self.copy("O", "x", 0, k).start()
        elif stage == "y":
            self.copy(which, "c", 1, k).start()
            if which == "A":
                self.copy("O", "x", 1, k).start()
        elif stage == "x":
            self.copy("O", "c", dy, k).start()

    EVENTS = ("Az01", "Az02", "Az03", "Ay00", "Ay01", "Ox01", "Dz01", "Ay02", "Ox02", "Dz02", "Ay03")
    EVENTS += ("Ox03", "Dz03", "Ox10", "Dy00", "Dy01", "Ox11", "Dy02", "Ox12", "Dy03", "Ox13")

    @staticmethod
    def parse(e):
        return e[0], e[1], int(e[2]), int(e[3])

    def all_core(self):
        for which in "AOD":
            for dy in range(2):
                for k in range(4):
                    self.copy(which, "c", dy, k).wait_recv()

    def all_sent(self):
        for which in "AD":
            for k in (1, 2, 3):
                self.copy(which, "z", 0, k).wait_send()
            for k in range(4):
                self.copy(which, "y", 0, k).wait_send()
        for dy in range(2):
            for k in range(4):
                if dy or k:
                    self.copy("O", "x", dy, k).wait_send()
                for which in "AOD":
                    self.copy(which, "c", dy, k).wait_send()


def forward_kernel(
    gu, wd, x, full0, down0, full1, down1, gate_out, up_out, hid_out, a_out, h_out,
    wg_s, wu_s, wd_s, hid_s, own_gu, own_d, send, recv, local,
):
    i = pl.program_id(0)
    steps = T // TILE
    y, z, c, xx = place()
    g0 = Gather(0, 0, gu, wd, full0, down0, send, recv)
    g1 = Gather(64, 1, gu, wd, full1, down1, send, recv)

    @pl.when(i == 0)
    def _():
        barrier = pltpu.get_barrier_semaphore()
        peers = meet(barrier) + [{"rep": 1 - xx}]
        for peer in peers:
            pl.semaphore_signal(barrier, inc=1, device_id=peer, device_id_type=MESH)
        pl.semaphore_wait(barrier, len(peers))
        g0.begin()
        ins = [pltpu.make_async_copy(gu, own_gu, local.at[0]), pltpu.make_async_copy(wd, own_d, local.at[1])]
        for one in ins:
            one.start()
        for one in ins:
            one.wait()
        me = number(y, z, c)
        outs = []
        for l, (full, down) in enumerate(((full0, down0), (full1, down1))):
            for m in range(2):
                outs.append(pltpu.make_async_copy(own_gu.at[m, l], full.at[m, me], local.at[2 + 3 * l + m]))
            outs.append(pltpu.make_async_copy(own_d.at[l], down.at[pl.ds(me * RD, RD), :], local.at[4 + 3 * l]))
        for one in outs:
            one.start()
        for e in Gather.EVENTS:
            g0.passed_on(Gather.parse(e))
            if e == "Dz03":
                g1.begin()
        for one in outs:
            one.wait()
        g0.all_core()
        loads = [
            pltpu.make_async_copy(full0.at[0], wg_s, local.at[0]),
            pltpu.make_async_copy(full0.at[1], wu_s, local.at[1]),
            pltpu.make_async_copy(down0, wd_s, local.at[2]),
        ]
        for one in loads:
            one.start()
        for one in loads:
            one.wait()

    wide = x[...].astype(WIDE)
    a_wide = (wide * norm_scale(wide)).astype(BF)
    a_out[...] = jnp.swapaxes(a_wide.astype(WIDE), 0, 1).astype(BF)

    total = jnp.zeros((TILE, D), WIDE)
    for at, size in CHUNKS:
        gate = dot(a_wide, wg_s[:, :, at : at + size].reshape(D, size))
        up = dot(a_wide, wu_s[:, :, at : at + size].reshape(D, size))
        gate_out[:, at : at + size] = gate
        up_out[:, at : at + size] = up
        hid = gate * (1.0 / (1.0 + jnp.exp(-gate))) * up
        hid_s[at : at + size, :] = jnp.swapaxes(hid, 0, 1)
        total = total + dot(hid.astype(BF), wd_s[at : at + size, :])
    put_hidden(hid_s, hid_out)
    h_out[...] = (wide + total.astype(BF).astype(WIDE)).astype(BF)

    for t in range(steps):
        mine = Gather.EVENTS[t * 3 : t * 3 + 3]

        @pl.when(i == t)
        def _():
            for e in mine:
                g1.passed_on(Gather.parse(e))
            if t == steps - 1:
                g1.all_core()
                g0.all_sent()
                g1.all_sent()


def forward(x, w_gate, w_up, w_down):
    steps = T // TILE
    gu = jnp.stack([w_gate, w_up])
    full = jax.ShapeDtypeStruct((2, 16, RG, FF), BF)
    down = jax.ShapeDtypeStruct((FF, D), BF)
    rows = lambda n: pl.BlockSpec((TILE, n), lambda i: (i, 0))
    return pl.pallas_call(
        forward_kernel,
        grid=(steps,),
        in_specs=[ANY, ANY, rows(D)],
        out_specs=[ANY] * 4
        + [rows(FF), rows(FF), pl.BlockSpec((16, PAD, TILE), lambda i: (0, 0, i)), pl.BlockSpec((D, TILE), lambda i: (0, i)), rows(D)],
        out_shape=[full, down, full, down]
        + [jax.ShapeDtypeStruct((T, FF), WIDE)] * 2
        + [jax.ShapeDtypeStruct((16, PAD, T), BF), jax.ShapeDtypeStruct((D, T), BF), jax.ShapeDtypeStruct((T, D), BF)],
        scratch_shapes=[
            VMEM((16, RG, FF), BF),
            VMEM((16, RG, FF), BF),
            VMEM((FF, D), BF),
            VMEM((FF, TILE), WIDE),
            VMEM((2, 2, RG, FF), BF),
            VMEM((2, RD, D), BF),
            pltpu.SemaphoreType.DMA((128,)),
            pltpu.SemaphoreType.DMA((128,)),
            pltpu.SemaphoreType.DMA((8,)),
        ],
        compiler_params=pltpu.CompilerParams(
            collective_id=0, has_side_effects=True, vmem_limit_bytes=ROOM, dimension_semantics=("arbitrary",)
        ),
        name="forward",
    )(gu, w_down, x)


def turn_kernel(h, dy, gu, wd, hid_out, a_out, dg_out, du_out, hid_s):
    wide = h[...].astype(WIDE)
    a = (wide * norm_scale(wide)).astype(BF)
    a_out[...] = jnp.swapaxes(a.astype(WIDE), 0, 1).astype(BF)
    for at, size in CHUNKS:
        gate = dot(a, gu[0, :, at : at + size])
        up = dot(a, gu[1, :, at : at + size])
        back = dot(dy[...], wd[at : at + size, :], ((1,), (1,))).astype(BF).astype(WIDE)
        sig = 1.0 / (1.0 + jnp.exp(-gate))
        act = gate * sig
        hid_s[at : at + size, :] = jnp.swapaxes(act * up, 0, 1)
        du_out[:, at : at + size] = (back * act).astype(BF)
        dg_out[:, at : at + size] = (back * up * (sig + act * (1.0 - sig))).astype(BF)
    put_hidden(hid_s, hid_out)


def once(shape):
    return pl.BlockSpec(shape, lambda i: (0,) * len(shape), pipeline_mode=pl.Buffered(1))


def turn(h, dy, full, down):
    rows = lambda n: pl.BlockSpec((TILE, n), lambda i: (i, 0))
    return pl.pallas_call(
        turn_kernel,
        grid=(T // TILE,),
        in_specs=[rows(D), rows(D), once((2, D, FF)), once((FF, D))],
        out_specs=[pl.BlockSpec((16, PAD, TILE), lambda i: (0, 0, i)), pl.BlockSpec((D, TILE), lambda i: (0, i)), rows(FF), rows(FF)],
        out_shape=[jax.ShapeDtypeStruct((16, PAD, T), BF), jax.ShapeDtypeStruct((D, T), BF)] + [jax.ShapeDtypeStruct((T, FF), BF)] * 2,
        scratch_shapes=[VMEM((FF, TILE), WIDE)],
        compiler_params=pltpu.CompilerParams(vmem_limit_bytes=ROOM, dimension_semantics=("arbitrary",)),
        name="turn",
    )(h, dy, full.reshape(2, D, FF), down)


def back_tile(dg, du, h, dy, gu, out):
    da = dot(dg, gu[0], ((1,), (1,))).astype(BF).astype(WIDE) + dot(du, gu[1], ((1,), (1,))).astype(BF).astype(WIDE)
    da = da.astype(BF).astype(WIDE)
    wide = h.astype(WIDE)
    scale = norm_scale(wide)
    along = jnp.sum(da * wide, -1, keepdims=True)
    by_h = da * scale - wide * (scale * scale * scale * along * (1.0 / D))
    out[...] = (dy.astype(WIDE) + by_h.astype(BF).astype(WIDE)).astype(BF)


def through_tile(dy, gate_in, up_in, wd, dg_out, du_out):
    for at, size in CHUNKS:
        gate, up = gate_in[:, at : at + size], up_in[:, at : at + size]
        back = dot(dy[...], wd[at : at + size, :], ((1,), (1,))).astype(BF).astype(WIDE)
        sig = 1.0 / (1.0 + jnp.exp(-gate))
        act = gate * sig
        du_out[:, at : at + size] = (back * act).astype(BF)
        dg_out[:, at : at + size] = (back * up * (sig + act * (1.0 - sig))).astype(BF)


ORDER = (3, 2, 1, 0)


AFTER_PRODUCT = {3: (0,), 5: (1,), 7: (2,), 9: (4,), 10: (3,), 11: (5,)}
AFTER_BACK = {0: (6,), 4: (8,), 5: (7,), 7: (9,)}
AFTER_THROUGH = {0: (10,), 5: (11,)}


def scatter_kernel(more, *refs):
    hid, a, dy, dg, du = refs[:5]
    refs = refs[5:]
    if more:
        h, gu, wd, gate, up = refs[:5]
        refs = refs[5:]
    gg_out, gu_out, gd_out = refs[:3]
    refs = refs[3:]
    if more:
        dh_out, dg_out, du_out = refs[:3]
        refs = refs[3:]
    own, own_d, r1, r1_d, cs, cs_d, r2, r2_d, r3, r3_d, send, recv, local, tiled = refs
    y, z, c, _ = place()
    barrier = pltpu.get_barrier_semaphore()
    peers = meet(barrier)
    for peer in peers:
        pl.semaphore_signal(barrier, inc=1, device_id=peer, device_id_type=MESH)

    def bufs(s):
        m, k = s // 4, ORDER[s % 4]
        if m == 0:
            return own_d.at[k], r1_d.at[k], cs_d.at[s % 2], r2_d.at[k], (r3_d.at[k - 1] if k else None)
        j = (m - 1) * 4 + k
        return own.at[j], r1.at[j], cs.at[s % 2], r2.at[j], (r3.at[(m - 1) * 3 + k - 1] if k else None)

    def remote(src, dst, sem, peer):
        return pltpu.make_async_remote_copy(
            src_ref=src, dst_ref=dst, send_sem=send.at[sem], recv_sem=recv.at[sem], device_id=peer, device_id_type=MESH
        )

    def by_core(s):
        _, one, out, _, _ = bufs(s)
        return remote(out, one, s, {"dp": number(y, z, 1 - c)})

    def by_y(s):
        mine, _, _, two, _ = bufs(s)
        return remote(mine.at[1], two, 12 + s, {"dp": number(1 - y, z, c)})

    def by_z(s):
        mine, _, _, _, three = bufs(s)
        return remote(mine.at[0], three, 24 + s, {"dp": number(y, xor4(z, ORDER[s % 4]), c)})

    def lhs_copies(s, lhs, lhs_d):
        m, k = s // 4, ORDER[s % 4]
        src, dst = (hid, lhs_d) if m == 0 else (a, lhs)
        out = []
        for dy_ in range(2):
            for dc in range(2):
                b = number(flip(y) if dy_ else y, xor4(z, k), flip(c) if dc else c)
                sem = 4 * (s % 2) + dy_ * 2 + dc
                rows = PAD if m == 0 else RG
                out.append(pltpu.make_async_copy(src.at[b], dst.at[s % 2, pl.ds((dy_ * 2 + dc) * rows, rows), :], local.at[sem]))
        return out

    def widths(m):
        return (256, 4) if m == 0 else (640, 5)

    def product(s, left, right):
        m = s // 4
        rows, r = (PAD, RD) if m == 0 else (RG, RG)
        mine, _, out, _, _ = bufs(s)
        size, n = widths(m)

        def body(j, _):
            cols = pl.ds(pl.multiple_of(j * size, size), size)
            p = dot(left[s % 2], right[:, cols])
            for dy_ in range(2):
                mine[dy_, :, cols] = p[(dy_ * 2) * rows : (dy_ * 2) * rows + r].astype(BF)
                out[dy_, :, cols] = p[(dy_ * 2 + 1) * rows : (dy_ * 2 + 1) * rows + r].astype(BF)
            return 0

        lax.fori_loop(0, n, body, 0)

    def each(m, fn):
        size, n = widths(m)

        def body(j, _):
            fn(pl.ds(pl.multiple_of(j * size, size), size))
            return 0

        lax.fori_loop(0, n, body, 0)

    def to_y(s):
        mine, one, _, _, _ = bufs(s)
        by_core(s).wait_recv()

        def fn(cols):
            mine[1, :, cols] = (mine[1, :, cols].astype(WIDE) + one[1, :, cols].astype(WIDE)).astype(BF)

        each(s // 4, fn)
        by_y(s).start()

    def to_z(s):
        m, k = s // 4, ORDER[s % 4]
        mine, one, _, two, _ = bufs(s)
        by_y(s).wait_recv()
        if k:

            def fn(cols):
                mine[0, :, cols] = (
                    mine[0, :, cols].astype(WIDE) + one[0, :, cols].astype(WIDE) + two[:, cols].astype(WIDE)
                ).astype(BF)

            each(m, fn)
            by_z(s).start()
            return
        threes = []
        for t in range(4 * m, 4 * m + 3):
            by_z(t).wait_recv()
            threes.append(bufs(t)[4])
        result = (gd_out, gg_out, gu_out)[m]

        def fn(cols):
            total = mine[0, :, cols].astype(WIDE) + one[0, :, cols].astype(WIDE) + two[:, cols].astype(WIDE)
            for three in threes:
                total = total + three[:, cols].astype(WIDE)
            result[:, cols] = total.astype(BF)

        each(m, fn)

    def products(rhs, rhs_d, lhs, lhs_d):
        right_d = pltpu.make_async_copy(dy, rhs_d, local.at[8])
        right_g = pltpu.make_async_copy(dg, rhs, local.at[9])
        right_u = pltpu.make_async_copy(du, rhs, local.at[9])
        for one in lhs_copies(0, lhs, lhs_d):
            one.start()
        right_d.start()
        right_g.start()
        pl.semaphore_wait(barrier, len(peers))
        for s in range(12):
            for one in lhs_copies(s, lhs, lhs_d):
                one.wait()
            if s + 1 < 12:
                for one in lhs_copies(s + 1, lhs, lhs_d):
                    one.start()
            if s == 0:
                right_d.wait()
            if s == 4:
                right_g.wait()
            if s == 8:
                right_u.wait()
            if s >= 2:
                by_core(s - 2).wait_send()
            product(s, lhs_d if s < 4 else lhs, rhs_d if s < 4 else rhs)
            if s == 7:
                right_u.start()
            by_core(s).start()
            if s >= 1:
                to_y(s - 1)
            for q in AFTER_PRODUCT.get(s, ()):
                to_z(q)

    def tiles(ins, outs, compute, after):
        n = T // TILE

        def copies(pairs, j, base, inward):
            out = []
            for i, (far, near) in enumerate(pairs):
                rows = far.at[pl.ds(pl.multiple_of(j * TILE, TILE), TILE), :]
                slot = near.at[j % 2]
                sem = tiled.at[base + 2 * i + j % 2]
                out.append(pltpu.make_async_copy(rows, slot, sem) if inward else pltpu.make_async_copy(slot, rows, sem))
            return out

        for one in copies(ins, 0, 0, True):
            one.start()

        def body(j, _):
            @pl.when(j + 1 < n)
            def _():
                for one in copies(ins, j + 1, 0, True):
                    one.start()

            for one in copies(ins, j, 0, True):
                one.wait()

            @pl.when(j >= 2)
            def _():
                for one in copies(outs, j - 2, 10, False):
                    one.wait()

            compute(j % 2)
            for one in copies(outs, j, 10, False):
                one.start()
            for t, which in after.items():

                @pl.when(j == t)
                def _():
                    for q in which:
                        to_z(q)

            return 0

        lax.fori_loop(0, n, body, 0)
        for j in (n - 2, n - 1):
            for one in copies(outs, j, 10, False):
                one.wait()

    def back_tiles(w, dg_s, du_s, h_s, dy_s, dh_s):
        load = pltpu.make_async_copy(gu, w, local.at[8])
        load.start()
        to_y(11)
        load.wait()

        def compute(i):
            back_tile(dg_s[i], du_s[i], h_s[i], dy_s[i], w, dh_s.at[i])

        tiles(((dg, dg_s), (du, du_s), (h, h_s), (dy, dy_s)), ((dh_out, dh_s),), compute, AFTER_BACK)

    def through_tiles(w, dh_s, gate_s, up_s, dg_s, du_s):
        load = pltpu.make_async_copy(wd, w, local.at[8])
        load.start()
        load.wait()

        def compute(i):
            through_tile(dh_s.at[i], gate_s.at[i], up_s.at[i], w, dg_s.at[i], du_s.at[i])

        tiles(((dh_out, dh_s), (gate, gate_s), (up, up_s)), ((dg_out, dg_s), (du_out, du_s)), compute, AFTER_THROUGH)

    pl.run_scoped(products, VMEM((T, FF), BF), VMEM((T, D), BF), VMEM((2, 4 * RG, T), BF), VMEM((2, 4 * PAD, T), BF))
    if more:
        wide_s, wide32_s, thin_s = VMEM((2, TILE, FF), BF), VMEM((2, TILE, FF), WIDE), VMEM((2, TILE, D), BF)
        pl.run_scoped(back_tiles, VMEM((2, D, FF), BF), wide_s, wide_s, thin_s, thin_s, thin_s)
        pl.run_scoped(through_tiles, VMEM((FF, D), BF), thin_s, wide32_s, wide32_s, wide_s, wide_s)
    else:
        to_y(11)
        for q in (6, 8, 7, 9, 10, 11):
            to_z(q)
    for s in range(12):
        if s >= 10:
            by_core(s).wait_send()
        by_y(s).wait_send()
        if ORDER[s % 4]:
            by_z(s).wait_send()


def scatter(ident, hid, a, dy, dg, du, more=()):
    vm = pl.BlockSpec(memory_space=pltpu.VMEM)
    outs = [jax.ShapeDtypeStruct((RG, FF), BF)] * 2 + [jax.ShapeDtypeStruct((RD, D), BF)]
    if more:
        outs += [jax.ShapeDtypeStruct((T, D), BF)] + [jax.ShapeDtypeStruct((T, FF), BF)] * 2
    return pl.pallas_call(
        functools.partial(scatter_kernel, bool(more)),
        in_specs=[ANY] * (5 + len(more)),
        out_specs=[vm] * 3 + ([ANY] * 3 if more else []),
        out_shape=outs,
        scratch_shapes=[
            VMEM((8, 2, RG, FF), BF),
            VMEM((4, 2, RD, D), BF),
            VMEM((8, 2, RG, FF), BF),
            VMEM((4, 2, RD, D), BF),
            VMEM((2, 2, RG, FF), BF),
            VMEM((2, 2, RD, D), BF),
            VMEM((8, RG, FF), BF),
            VMEM((4, RD, D), BF),
            VMEM((6, RG, FF), BF),
            VMEM((3, RD, D), BF),
            pltpu.SemaphoreType.DMA((36,)),
            pltpu.SemaphoreType.DMA((36,)),
            pltpu.SemaphoreType.DMA((10,)),
            pltpu.SemaphoreType.DMA((16,)),
        ],
        compiler_params=pltpu.CompilerParams(collective_id=ident, has_side_effects=True, vmem_limit_bytes=ROOM),
        name="scatter",
    )(hid, a.reshape(16, RG, T), dy, dg, du, *more)


def solution(mesh):
    def step(x, dy, *arrays):
        weights, m, v = (arrays[i : i + 3] for i in (0, 3, 6))
        x, dy = x[0], dy[0]
        full0, down0, full1, down1, gate0, up0, hid0, a0, h1 = forward(x, *weights)
        hid1, a1, dg1, du1 = turn(h1, dy, full1, down1)
        more = (h1, full1.reshape(2, D, FF), down0, gate0, up0)
        gate_g1, up_g1, down_g1, dh1, dg0, du0 = scatter(1, hid1, a1, dy, dg1, du1, more)
        gate_g0, up_g0, down_g0 = scatter(2, hid0, a0, dh1, dg0, du0)
        gradients = [(gate_g0, gate_g1), (up_g0, up_g1), (down_g0, down_g1)]
        new = [
            adamw(w.astype(WIDE), m, v, jnp.stack([one.astype(WIDE) for one in g]))
            for w, m, v, g in zip(weights, m, v, gradients, strict=True)
        ]
        return tuple(one[which] for which in range(3) for one in new)

    states, cut = P(("rep", "dp"), None, None), P(None, "dp", None)
    return jax.shard_map(
        step,
        mesh=mesh,
        in_specs=(states, states) + (cut,) * 9,
        out_specs=(P("rep", "dp", None),) * 9,
        check_vma=False,
    )
```

time: 1070 us -> 553 us (0.52)
  waiting for transfers between devices: 628 us -> 0 us
  Pallas kernels: 0 us -> 529 us
  matrix products: 373 us -> 0 us
  local copies, waits for them, and re-layouts: 22 us -> 1.27 us
  between operations: 14.5 us -> 1.21 us
    pallas_call x0 -> x4, Pallas kernels: none -> 529 us  [the longest x2 292 us: scatter(): pl.pallas_call(functools.partial(scatter_kernel, bool(more)), in_specs=[A...]
    reduce_scatter x6 -> x0, waiting for transfers between devices: 377 us -> none  [step(): lax.psum_scatter(by_w[name], 'dp', scatter_dimension=0, tiled=True)]
    dot_general x15 -> x0, matrix products: 373 us -> none  [the longest x5 137 us: layer(): gate = jnp.dot(a, w['w_gate'], preferred_element_type=jnp.float32)]
    all_gather x6 -> x0, waiting for transfers between devices: 249 us -> none  [fetched(): lax.all_gather(w[number], 'dp', axis=0, tiled=True)]
    unnamed x32 -> x18, local copies, waits for them, and re-layouts: 15.8 us -> 1.27 us
  transfers between devices with their start and end apart: 12 -> 0, of which waited for: 11 -> 0; matrix products, arithmetic and copies ran while one was open for 28% -> 0% of each run, Pallas kernels for 0% -> 0%
where the time goes in v1:
time: 553 us; the launch traced here: 544 us
  Pallas kernels  529 us (96%)
  other arithmetic  12.8 us (2%)
    pallas_call x2, Pallas kernels, scatter(): pl.pallas_call(functools.partial(scatter_kernel, bool(more)), in_specs=[A...  292 us
    pallas_call x1, Pallas kernels, forward(): pl.pallas_call(forward_kernel, grid=(steps,), in_specs=[ANY, ANY, rows(D)...  181 us
    pallas_call x1, Pallas kernels, turn(): pl.pallas_call(turn_kernel, grid=(T // TILE,), in_specs=[rows(D), rows(D)...  56.1 us

profile of v1, /device:TPU:0, one launch (start us, length us, event | category | flops | bytes accessed | tf_op | source)
XLA Modules:
  0.0 544.5 jit_solution(4448717957324019062)
XLA Ops:
  0.6 2.7 pad_maximum_fusion.gu
  3.4 180.7 %forward.1 = (bf16[2,16,64,3200]{3,2,1,0:T(8,128)(2,1)}, bf16[3200,1024]{1,0:T(8,128)(2,1)}, bf16[2,16,64,3200]{3,2,1,0:T(8,128)(2,1)}, bf16[3200,1024]{1,0:T(8,...) custom-call(bf16[2,2,64,3200]{3,2,1,0:T(8,128)(2,1)} %pad_maximum_fu, ...), custom_call_target="tpu_custom_call" | custom-call | tf_op jit(solution)/shard_map/forward/pallas_call | solution.py:236
  184.1 56.1 %turn.1 = (bf16[16,208,2048]{2,1,0:T(8,128)(2,1)}, bf16[1024,2048]{1,0:T(8,128)(2,1)}, bf16[2048,3200]{1,0:T(8,128)(2,1)}, bf16[2048,3200]{1,0:T(8,128)(2,1)}) custom-call(bf16[2048,1024]{1,0:T(8,128)(2,1)} %get-tuple-element.32.h.refs_5_, bf16[2048,1024]{1,0:T(8,128)(2,1)} %bitcast.15, bf16[2,1024,3200]{2,1,0:T(8,128)(2,1)} %bitcast.13, ...), custom_call_target="tpu_custom_call" | custom-call | tf_op jit(solution)/shard_map/turn/pallas_call | solution.py:285
  240.2 162.9 %scatter.2 = (bf16[64,3200]{1,0:T(8,128)(2,1)}, bf16[64,3200]{1,0:T(8,128)(2,1)}, bf16[200,1024]{1,0:T(8,128)(2,1)}, bf16[2048,1024]{1,0:T(8,128)(2,1)}, bf16[20...) custom-call(bf16[16,208,2048]{2,1,0:T(8,128)(2,1)} %get-tuple-element.35.refs_0_, bf16[16,64,2048]{2,1,0:T(8,128)(2,1)} %bitcast.19, ...), custom_call_target="tpu_custom_call" | custom-call | tf_op jit(solution)/shard_map/scatter/pallas_call | solution.py:566
  403.1 0.0 copy-start
  403.1 129.5 %scatter.3 = (bf16[64,3200]{1,0:T(8,128)(2,1)}, bf16[64,3200]{1,0:T(8,128)(2,1)}, bf16[200,1024]{1,0:T(8,128)(2,1)}) custom-call(bf16[16,208,2048]{2,1,0:T(8,128)(2,1)} %get-tuple-element.30.refs_0_, bf16[16,64,2048]{2,1,0:T(8,128)(2,1)} %bitcast.17, bf16[2048,1024]{1,0:T(8,128)(2,1)} %get-tuple-element.42.refs_2_, ...), custom_call_target="tpu_custom_call" | custom-call | tf_op jit(solution)/shard_map/scatter/pallas_call | solution.py:566
  532.6 0.0 copy-done
  532.6 0.0 copy-start.1
  532.6 0.0 copy-start.2
  532.7 0.0 copy-start.3
  532.7 0.0 copy-start.4
  532.7 0.0 copy-start.5
  532.7 0.0 copy-start.6
  532.7 0.0 copy-start.7
  532.7 0.0 copy-start.8
  532.7 4.9 fusion.10
  537.6 0.0 copy-done.1
  537.6 0.0 copy-done.2
  537.6 0.0 copy-done.3
  537.6 0.0 copy-done.4
  537.7 0.0 copy-done.5
  537.7 1.1 copy-done.6
  538.8 0.0 copy-done.7
  538.8 0.1 copy-done.8
  538.9 5.2 fusion.2
Async XLA Ops:
  403.1 129.5 %copy-start = (bf16[2,200,1024]{2,1,0:T(8,128)(2,1)S(1)}, bf16[2,200,1024]{2,1,0:T(8,128)(2,1)}, u32[]{:S(2)}) copy-start(bf16[2,200,1024]{2,1,0:T(8,128)(2,1)} %wd.1) | copy-start | bytes 2457604
  532.6 5.0 copy-start.1
  532.6 5.0 copy-start.2
  532.7 5.0 copy-start.3
  532.7 5.0 copy-start.4
  532.7 5.0 copy-start.5
  532.7 6.1 %copy-start.6 = (f32[2,64,3200]{2,1,0:T(8,128)S(1)}, f32[2,64,3200]{2,1,0:T(8,128)}, u32[]{:S(2)}) copy-start(f32[2,64,3200]{2,1,0:T(8,128)} %param.17) | copy-start | bytes 4915204
  532.7 6.1 %copy-start.7 = (bf16[64,3200]{1,0:T(8,128)(2,1)S(1)}, bf16[64,3200]{1,0:T(8,128)(2,1)}, u32[]{:S(2)}) copy-start(bf16[64,3200]{1,0:T(8,128)(2,1)} %get-tuple-element.46) | copy-start | bytes 1228804
  532.7 6.2 %copy-start.8 = (bf16[64,3200]{1,0:T(8,128)(2,1)S(1)}, bf16[64,3200]{1,0:T(8,128)(2,1)}, u32[]{:S(2)}) copy-start(bf16[64,3200]{1,0:T(8,128)(2,1)} %get-tuple-element.48) | copy-start | bytes 1228804
